TPU v7x, 32 devices: a 4x4x1 block of a 4x4x8 slice. The times are simulated.
32 devices in a mesh: dp: 1 (over z), sp: 32 (over y, x, core).
Axes of the slice: x: 4, y: 4, z: 1, core: 2. Of those that a mesh axis runs over, the one named last changes fastest.
The devices are a block of a 4x4x8 slice.
Arguments:
- latent: bfloat16 [16, 128, 128, 4], P('dp', 'sp')
- time_emb: bfloat16 [16, 1280], P('dp')
- w_in: bfloat16 [3, 3, 4, 320], replicated
- b_in: bfloat16 [320], replicated
- gn1_scale: bfloat16 [2, 320], replicated
- gn1_shift: bfloat16 [2, 320], replicated
- conv1_w: bfloat16 [2, 3, 3, 320, 320], replicated
- conv1_b: bfloat16 [2, 320], replicated
- temb_w: bfloat16 [2, 1280, 320], replicated
- temb_b: bfloat16 [2, 320], replicated
- gn2_scale: bfloat16 [2, 320], replicated
- gn2_shift: bfloat16 [2, 320], replicated
- conv2_w: bfloat16 [2, 3, 3, 320, 320], replicated
- conv2_b: bfloat16 [2, 320], replicated
- down_w: bfloat16 [3, 3, 320, 320], replicated
- down_b: bfloat16 [320], replicated
Outputs:
- output 1: bfloat16 [16, 128, 128, 320], P('dp', 'sp')
- output 2: bfloat16 [16, 128, 128, 320], P('dp', 'sp')
- output 3: bfloat16 [16, 128, 128, 320], P('dp', 'sp')
- output 4: bfloat16 [16, 64, 64, 320], P('dp', 'sp')
All inputs are finite; a program needn't handle non-finite values.
Results may differ from a plain program's by a relative error of at most 0.0134259.
Values are sent between devices in bfloat16 or wider.
A program may use at most 768 MiB of HBM per device.

v0:
```python
import jax
import jax.numpy as jnp
from jax import lax
from jax.sharding import PartitionSpec as P

GN_GROUPS = 32
GN_EPS = 1e-5
DIM_NUMS = ("NHWC", "HWIO", "NHWC")


def conv_valid_rows(inputs, kernel, bias_c, stride):
    out_f32 = lax.conv_general_dilated(inputs, kernel, (stride, stride), ((0, 0), (1, 1)), dimension_numbers=DIM_NUMS, preferred_element_type=jnp.float32)
    return (out_f32 + bias_c.astype(jnp.float32)).astype(jnp.bfloat16)


def group_sums(values):
    batch_n, rows_n, cols_n, chan_n = values.shape
    grouped = values.reshape(batch_n, rows_n * cols_n, GN_GROUPS, chan_n // GN_GROUPS)
    return jnp.stack([grouped.sum(axis=(1, 3)), jnp.square(grouped).sum(axis=(1, 3))], axis=-1)


def norm_silu(values, sums_all, elem_count, gain_c, shift_c):
    group_ch = values.shape[-1] // GN_GROUPS
    grp_mean = sums_all[..., 0] / elem_count
    grp_var = sums_all[..., 1] / elem_count - grp_mean * grp_mean
    inv_std = lax.rsqrt(grp_var + GN_EPS)
    scale_bc = jnp.repeat(inv_std, group_ch, axis=1) * gain_c.astype(jnp.float32)
    offset_bc = shift_c.astype(jnp.float32) - jnp.repeat(grp_mean, group_ch, axis=1) * scale_bc
    return jax.nn.silu(values * scale_bc[:, None, None, :] + offset_bc[:, None, None, :]).astype(jnp.bfloat16)


def solution(mesh):
    sp_size = mesh.shape["sp"]
    to_next = [(device, device + 1) for device in range(sp_size - 1)]
    to_prev = [(device + 1, device) for device in range(sp_size - 1)]

    def row_from_above(band_block):
        return lax.ppermute(band_block[:, -1:], "sp", to_next)

    def row_from_below(band_block):
        return lax.ppermute(band_block[:, :1], "sp", to_prev)

    def conv_band(band_block, kernel, bias_c):
        padded = jnp.concatenate([row_from_above(band_block), band_block, row_from_below(band_block)], axis=1)
        return conv_valid_rows(padded, kernel, bias_c, 1)

    def band_program(latent, time_emb, w_in, b_in, gn1_scale, gn1_shift, conv1_w, conv1_b, temb_w, temb_b, gn2_scale, gn2_shift, conv2_w, conv2_b, down_w, down_b):
        elem_count = latent.shape[1] * sp_size * latent.shape[2] * (w_in.shape[-1] // GN_GROUPS)
        emb_act = jax.nn.silu(time_emb.astype(jnp.float32)).astype(jnp.bfloat16)
        hidden = conv_band(latent, w_in, b_in)
        outputs = [hidden]
        for layer_idx in range(conv1_w.shape[0]):
            hidden_f32 = hidden.astype(jnp.float32)
            sums_all = lax.psum(group_sums(hidden_f32), "sp")
            normed = norm_silu(hidden_f32, sums_all, elem_count, gn1_scale[layer_idx], gn1_shift[layer_idx])
            branch = conv_band(normed, conv1_w[layer_idx], conv1_b[layer_idx])
            emb_proj = jnp.dot(emb_act, temb_w[layer_idx], preferred_element_type=jnp.float32) + temb_b[layer_idx].astype(jnp.float32)
            mixed_in = branch.astype(jnp.float32) + emb_proj[:, None, None, :]
            sums_all = lax.psum(group_sums(mixed_in), "sp")
            normed = norm_silu(mixed_in, sums_all, elem_count, gn2_scale[layer_idx], gn2_shift[layer_idx])
            branch = conv_band(normed, conv2_w[layer_idx], conv2_b[layer_idx])
            hidden = (hidden_f32 + branch.astype(jnp.float32)).astype(jnp.bfloat16)
            outputs.append(hidden)
        padded = jnp.concatenate([row_from_above(hidden), hidden], axis=1)
        outputs.append(conv_valid_rows(padded, down_w, down_b, 2))
        return tuple(outputs)

    band_spec = P("dp", "sp", None, None)
    return jax.shard_map(band_program, mesh=mesh, in_specs=(band_spec, P("dp", None)) + (P(),) * 14, out_specs=(band_spec,) * 4, check_vma=False)
```

profile of v0, /device:TPU:97, one launch (start us, length us, event | category | flops | bytes accessed | tf_op | source)
XLA Modules:
  0.0 549.7 jit_solution(18411070348942686495)
XLA Ops:
  1.7 4.6 collective-permute-start
  12.8 7.1 %convert_reduce_fusion.1 = (f32[16,320]{1,0:T(8,128)S(1)}, f32[16,320]{1,0:T(8,128)S(1)}, bf16[16,4,128,320]{3,0,2,1:T(8,128)(2,1)}) fusion(f32[320]{0:T(512)S(1)} %convert_element_type.126, bf16[3,3,4,320]{3,2,1,0:T(4,128)(2,1)} %param.18, bf16[16,1,128,4]{0,3,2,1:T(4,128)(2,1)S(1)} %collective-permute-done.1, bf16[16,4,128,4]{0,3,2,1:T(4,128)(2,1)S(1)} %copy.62, ...), kind=kOutput, calls=%fused_computation.7 | convolution fusion | flops 203773952 | bytes 5406464 | tf_op jit(solution)/shard_map/conv_general_dilated | solution.py:12
  20.7 48.7 %psum.28 = f32[16,32,2]{1,0,2:T(8,128)S(1)} all-reduce(f32[16,32,2]{1,0,2:T(8,128)S(1)} %pad_maximum_fusion), channel_id=1, replica_groups=mesh['dp'=1,'sp'=32] {'sp'}, use_global_device_ids=true, to_apply=%region_4.5 | all-reduce | flops 1024 | bytes 8192 | tf_op jit(solution)/shard_map/psum | solution.py:54
  70.1 5.7 %fusion.7 = bf16[16,4,128,320]{3,0,2,1:T(8,128)(2,1)S(1)} fusion(bf16[16,4,128,320]{3,0,2,1:T(8,128)(2,1)} %get-tuple-element.60, f32[16,320]{1,0:T(8,128)S(1)} %get-tuple-element.48, f32[16,320]{1,0:T(8,128)S(1)} %get-tuple-element.49), kind=kLoop, calls=%fused_computation.15 | loop fusion | flops 20971520 | bytes 10526720 | tf_op jit(solution)/shard_map/convert_element_type | solution.py:29
  82.4 3.4 collective-permute-start.2
  94.2 6.2 %collective-permute-done.2 = bf16[16,1,128,320]{2,3,1,0:T(8,128)(2,1)} collective-permute-done((bf16[16,1,128,320]{2,3,1,0:T(8,128)(2,1)S(1)}, bf16[16,1,128,320]{2,3,1,0:T(8,128)(2,1)}, u32[]{:S(2)}, u32[]{:S(2)}) %collective-permute-start.2) | collective-permute-done | bytes 1310752 | tf_op jit(solution)/shard_map/ppermute | solution.py:38
  103.2 4.3 collective-permute-done.3
  107.5 2.9 copy.66
  110.4 31.4 %fusion.19 = (f32[16,320]{1,0:T(8,128)S(1)}, f32[16,320]{1,0:T(8,128)S(1)}, bf16[16,4,128,320]{3,0,2,1:T(8,128)(2,1)}) fusion(f32[16,320]{1,0:T(8,128)S(1)} %convolution_add_fusion.1, f32[320]{0:T(512)} %get-tuple-element.39, bf16[2,3,3,320,320]{4,3,2,1,0:T(8,128)(2,1)} %param.22, bf16[16,1,128,320]{3,0,2,1:T(8,128)(2,1)} %copy.66, ...), kind=kOutput, calls=%fused_computation.36 | convolution fusion | flops 15062784000 | bytes 16955392 | tf_op jit(solution)/shard_map/conv_general_dilated | solution.py:12
  142.6 47.0 %psum.29 = f32[16,32,2]{1,0,2:T(8,128)S(1)} all-reduce(f32[16,32,2]{1,0,2:T(8,128)S(1)} %pad_maximum_fusion.1), channel_id=1, replica_groups=mesh['dp'=1,'sp'=32] {'sp'}, use_global_device_ids=true, to_apply=%region_9.10 | all-reduce | flops 1024 | bytes 8192 | tf_op jit(solution)/shard_map/psum | solution.py:59
  190.2 5.9 %multiply_convert_fusion.1 = bf16[16,4,128,320]{3,0,2,1:T(8,128)(2,1)S(1)} fusion(bf16[16,4,128,320]{3,0,2,1:T(8,128)(2,1)} %get-tuple-element.61, f32[16,320]{1,0:T(8,128)S(1)} %get-tuple-element.46, f32[16,320]{1,0:T(8,128)S(1)} %get-tuple-element.47, f32[16,320]{1,0:T(8,128)S(1)} %convolution_add_fusion.1), kind=kLoop, calls=%fused_computation.33 | loop fusion | flops 23592960 | bytes 10547200 | tf_op jit(solution)/shard_map/convert_element_type | solution.py:29
  202.8 3.7 collective-permute-start.4
  211.3 9.8 %collective-permute-done.4 = bf16[16,1,128,320]{2,3,1,0:T(8,128)(2,1)} collective-permute-done((bf16[16,1,128,320]{2,3,1,0:T(8,128)(2,1)S(1)}, bf16[16,1,128,320]{2,3,1,0:T(8,128)(2,1)}, u32[]{:S(2)}, u32[]{:S(2)}) %collective-permute-start.4) | collective-permute-done | bytes 1310752 | tf_op jit(solution)/shard_map/ppermute | solution.py:38
  223.9 4.3 collective-permute-done.5
  231.1 32.3 %convert_reduce_fusion = (f32[16,320]{1,0:T(8,128)S(1)}, f32[16,320]{1,0:T(8,128)S(1)}, bf16[16,4,128,320]{3,0,2,1:T(8,128)(2,1)}) fusion(f32[320]{0:T(512)S(1)} %get-tuple-element.41, bf16[2,3,3,320,320]{4,3,2,1,0:T(8,128)(2,1)} %param.28, bf16[16,1,128,320]{3,0,2,1:T(8,128)(2,1)} %copy.70, bf16[16,4,128,320]{3,0,2,1:T(8,128)(2,1)} %copy-done.3, ...), kind=kOutput, calls=%fused_computation.3 | convolution fusion | flops 15070648320 | bytes 23225600 | tf_op jit(solution)/shard_map/conv_general_dilated | solution.py:12
  264.3 46.8 %psum.30 = f32[16,32,2]{1,0,2:T(8,128)S(1)} all-reduce(f32[16,32,2]{1,0,2:T(8,128)S(1)} %pad_maximum_fusion.2), channel_id=1, replica_groups=mesh['dp'=1,'sp'=32] {'sp'}, use_global_device_ids=true, to_apply=%region_14.15 | all-reduce | flops 1024 | bytes 8192 | tf_op jit(solution)/shard_map/psum | solution.py:54
  311.7 5.7 %fusion.16 = bf16[16,4,128,320]{3,0,2,1:T(8,128)(2,1)S(1)} fusion(bf16[16,4,128,320]{3,0,2,1:T(8,128)(2,1)} %get-tuple-element.62, f32[16,320]{1,0:T(8,128)S(1)} %get-tuple-element.44, f32[16,320]{1,0:T(8,128)S(1)} %get-tuple-element.45), kind=kLoop, calls=%fused_computation.24 | loop fusion | flops 20971520 | bytes 10526720 | tf_op jit(solution)/shard_map/convert_element_type | solution.py:29
  324.0 3.7 collective-permute-start.6
  333.9 8.3 %collective-permute-done.6 = bf16[16,1,128,320]{2,3,1,0:T(8,128)(2,1)} collective-permute-done((bf16[16,1,128,320]{2,3,1,0:T(8,128)(2,1)S(1)}, bf16[16,1,128,320]{2,3,1,0:T(8,128)(2,1)}, u32[]{:S(2)}, u32[]{:S(2)}) %collective-permute-start.6) | collective-permute-done | bytes 1310752 | tf_op jit(solution)/shard_map/ppermute | solution.py:38
  345.1 4.3 collective-permute-done.7
  352.3 31.4 %fusion.18 = (f32[16,320]{1,0:T(8,128)S(1)}, f32[16,320]{1,0:T(8,128)S(1)}, bf16[16,4,128,320]{3,0,2,1:T(8,128)(2,1)}) fusion(f32[16,320]{1,0:T(8,128)S(1)} %convolution_add_fusion, f32[320]{0:T(512)S(1)} %copy-done.15, bf16[2,3,3,320,320]{4,3,2,1,0:T(8,128)(2,1)} %param.22, bf16[16,1,128,320]{3,0,2,1:T(8,128)(2,1)} %copy.74, ...), kind=kOutput, calls=%fused_computation.30 | convolution fusion | flops 15062784000 | bytes 16954624 | tf_op jit(solution)/shard_map/conv_general_dilated | solution.py:12
  384.5 46.8 %psum.31 = f32[16,32,2]{1,0,2:T(8,128)S(1)} all-reduce(f32[16,32,2]{1,0,2:T(8,128)S(1)} %pad_maximum_fusion.3), channel_id=1, replica_groups=mesh['dp'=1,'sp'=32] {'sp'}, use_global_device_ids=true, to_apply=%region_19.20 | all-reduce | flops 1024 | bytes 8192 | tf_op jit(solution)/shard_map/psum | solution.py:59
  432.0 5.9 %multiply_convert_fusion = bf16[16,4,128,320]{3,0,2,1:T(8,128)(2,1)S(1)} fusion(bf16[16,4,128,320]{3,0,2,1:T(8,128)(2,1)} %get-tuple-element.63, f32[16,320]{1,0:T(8,128)S(1)} %get-tuple-element.42, f32[16,320]{1,0:T(8,128)S(1)} %get-tuple-element.43, f32[16,320]{1,0:T(8,128)S(1)} %convolution_add_fusion), kind=kLoop, calls=%fused_computation.27 | loop fusion | flops 23592960 | bytes 10547200 | tf_op jit(solution)/shard_map/convert_element_type | solution.py:29
  444.6 3.7 collective-permute-start.8
  453.0 9.8 %collective-permute-done.8 = bf16[16,1,128,320]{2,3,1,0:T(8,128)(2,1)} collective-permute-done((bf16[16,1,128,320]{2,3,1,0:T(8,128)(2,1)S(1)}, bf16[16,1,128,320]{2,3,1,0:T(8,128)(2,1)}, u32[]{:S(2)}, u32[]{:S(2)}) %collective-permute-start.8) | collective-permute-done | bytes 1310752 | tf_op jit(solution)/shard_map/ppermute | solution.py:38
  465.7 4.3 collective-permute-done.9
  472.9 29.5 %fusion.17 = bf16[16,4,128,320]{3,0,2,1:T(8,128)(2,1)S(1)} fusion(bf16[16,4,128,320]{3,0,2,1:T(8,128)(2,1)} %get-tuple-element.62, f32[320]{0:T(512)S(1)} %get-tuple-element.40, bf16[16,1,128,320]{3,0,2,1:T(8,128)(2,1)} %copy.78, bf16[16,4,128,320]{3,0,2,1:T(8,128)(2,1)} %copy-done.4, bf16[16,1,128,320]{3,0,2,1:T(8,128)(2,1)} %copy.77, ...), kind=kOutput, calls=%fused_computation.25 | convolution fusion | flops 15060172800 | bytes 23184640 | tf_op jit(solution)/shard_map/conv_general_dilated | solution.py:12
  510.6 8.5 %copy.81 = bf16[16,4,128,320]{2,3,1,0:T(8,128)(2,1)} copy(bf16[16,4,128,320]{3,0,2,1:T(8,128)(2,1)} %get-tuple-element.60) | data formatting | bytes 10485760
  519.1 8.5 %copy.82 = bf16[16,4,128,320]{2,3,1,0:T(8,128)(2,1)} copy(bf16[16,4,128,320]{3,0,2,1:T(8,128)(2,1)} %get-tuple-element.62) | data formatting | bytes 10485760
  527.6 8.5 %copy.83 = bf16[16,4,128,320]{2,3,1,0:T(8,128)(2,1)} copy(bf16[16,4,128,320]{3,0,2,1:T(8,128)(2,1)} %copy-done.5) | data formatting | bytes 10485760
  536.0 2.9 copy.80
  538.9 8.8 %add_convert_fusion.5 = bf16[16,2,64,320]{3,0,2,1:T(8,128)(2,1)S(1)} fusion(bf16[3,3,320,320]{3,2,1,0:T(8,128)(2,1)S(1)} %copy-done, bf16[16,4,128,320]{3,0,2,1:T(8,128)(2,1)} %copy-done.5, bf16[16,1,128,320]{3,0,2,1:T(8,128)(2,1)} %copy.80, f32[320]{0:T(512)S(1)} %convert_element_type.154), kind=kOutput, calls=%fused_computation.67 | convolution fusion | flops 3769630720 | bytes 9708800 | tf_op jit(solution)/shard_map/conv_general_dilated | solution.py:12
  (126 shorter events, 93.3 us)
Async XLA Ops:
  0.6 538.3 %copy-start = (bf16[3,3,320,320]{3,2,1,0:T(8,128)(2,1)S(1)}, bf16[3,3,320,320]{3,2,1,0:T(8,128)(2,1)}, u32[]{:S(2)}) copy-start(bf16[3,3,320,320]{3,2,1,0:T(8,128)(2,1)} %param.30) | copy-start | bytes 5529604
  1.7 10.1 %collective-permute-start = (bf16[16,1,128,4]{0,3,2,1:T(4,128)(2,1)S(1)}, bf16[16,1,128,4]{0,3,2,1:T(4,128)(2,1)S(1)}, u32[]{:S(2)}, u32[]{:S(2)}) collective-permute-start(bf16[16,1,128,4]{0,3,2,1:T(4,128)(2,1)S(1)} %copy.60), channel_id=1, source_target_pairs={{0,1},{1,2},{2,3},{3,4},{4,5},{5,6},{6,7},{7,8},{8,9},{9,10},{10,1... | collective-permute-start | bytes 49160 | tf_op jit(solution)/shard_map/ppermute | solution.py:38
  6.5 6.3 %collective-permute-start.1 = (bf16[16,1,128,4]{0,3,2,1:T(4,128)(2,1)S(1)}, bf16[16,1,128,4]{0,3,2,1:T(4,128)(2,1)S(1)}, u32[]{:S(2)}, u32[]{:S(2)}) collective-permute-start(bf16[16,1,128,4]{0,3,2,1:T(4,128)(2,1)S(1)} %copy.61), channel_id=1, source_target_pairs={{1,0},{2,1},{3,2},{4,3},{5,4},{6,5},{7,6},{8,7},{9,8},{10,9},{11,1... | collective-permute-start | bytes 49160 | tf_op jit(solution)/shard_map/ppermute | solution.py:41
  75.7 2.7 copy-start.1
  78.4 12.5 %copy-start.10 = (bf16[2,320]{1,0:T(2,128)(2,1)S(1)}, bf16[2,320]{1,0:T(2,128)(2,1)}, u32[]{:S(2)}) copy-start(bf16[2,320]{1,0:T(2,128)(2,1)} %param.25) | copy-start | bytes 3844
  78.4 13.1 %copy-start.11 = (bf16[2,320]{1,0:T(2,128)(2,1)S(1)}, bf16[2,320]{1,0:T(2,128)(2,1)}, u32[]{:S(2)}) copy-start(bf16[2,320]{1,0:T(2,128)(2,1)} %param.23) | copy-start | bytes 3844
  78.4 13.7 %copy-start.12 = (bf16[2,320]{1,0:T(2,128)(2,1)S(1)}, bf16[2,320]{1,0:T(2,128)(2,1)}, u32[]{:S(2)}) copy-start(bf16[2,320]{1,0:T(2,128)(2,1)} %param.27) | copy-start | bytes 3844
  78.4 13.7 %copy-start.13 = (bf16[2,320]{1,0:T(2,128)(2,1)S(1)}, bf16[2,320]{1,0:T(2,128)(2,1)}, u32[]{:S(2)}) copy-start(bf16[2,320]{1,0:T(2,128)(2,1)} %param.26) | copy-start | bytes 3844
  82.4 17.9 %collective-permute-start.2 = (bf16[16,1,128,320]{2,3,1,0:T(8,128)(2,1)S(1)}, bf16[16,1,128,320]{2,3,1,0:T(8,128)(2,1)}, u32[]{:S(2)}, u32[]{:S(2)}) collective-permute-start(bf16[16,1,128,320]{2,3,1,0:T(8,128)(2,1)S(1)} %copy.63), channel_id=1, source_target_pairs={{0,1},{1,2},{2,3},{3,4},{4,5},{5,6},{6,7},{7,8},{8,9},{9,10},{10,1... | collective-permute-start | bytes 3932168 | tf_op jit(solution)/shard_map/ppermute | solution.py:38
  88.6 18.9 %collective-permute-start.3 = (bf16[16,1,128,320]{2,3,1,0:T(8,128)(2,1)}, bf16[16,1,128,320]{2,3,1,0:T(8,128)(2,1)}, u32[]{:S(2)}, u32[]{:S(2)}) collective-permute-start(bf16[16,1,128,320]{2,3,1,0:T(8,128)(2,1)} %copy.64), channel_id=1, source_target_pairs={{1,0},{2,1},{3,2},{4,3},{5,4},{6,5},{7,6},{8,7},{9,8},{10,9},{11,1... | collective-permute-start | bytes 3932168 | tf_op jit(solution)/shard_map/ppermute | solution.py:41
  196.2 2.6 copy-start.3
  198.8 12.5 %copy-start.14 = (bf16[2,320]{1,0:T(2,128)(2,1)S(1)}, bf16[2,320]{1,0:T(2,128)(2,1)}, u32[]{:S(2)}) copy-start(bf16[2,320]{1,0:T(2,128)(2,1)} %param.29) | copy-start | bytes 3844
  202.8 18.3 %collective-permute-start.4 = (bf16[16,1,128,320]{2,3,1,0:T(8,128)(2,1)S(1)}, bf16[16,1,128,320]{2,3,1,0:T(8,128)(2,1)}, u32[]{:S(2)}, u32[]{:S(2)}) collective-permute-start(bf16[16,1,128,320]{2,3,1,0:T(8,128)(2,1)S(1)} %copy.67), channel_id=1, source_target_pairs={{0,1},{1,2},{2,3},{3,4},{4,5},{5,6},{6,7},{7,8},{8,9},{9,10},{10,1... | collective-permute-start | bytes 3932168 | tf_op jit(solution)/shard_map/ppermute | solution.py:38
  209.3 18.9 %collective-permute-start.5 = (bf16[16,1,128,320]{2,3,1,0:T(8,128)(2,1)}, bf16[16,1,128,320]{2,3,1,0:T(8,128)(2,1)}, u32[]{:S(2)}, u32[]{:S(2)}) collective-permute-start(bf16[16,1,128,320]{2,3,1,0:T(8,128)(2,1)} %copy.68), channel_id=1, source_target_pairs={{1,0},{2,1},{3,2},{4,3},{5,4},{6,5},{7,6},{8,7},{9,8},{10,9},{11,1... | collective-permute-start | bytes 3932168 | tf_op jit(solution)/shard_map/ppermute | solution.py:41
  231.1 80.5 %copy-start.6 = (f32[320]{0:T(512)S(1)}, f32[320]{0:T(512)}, u32[]{:S(2)}) copy-start(f32[320]{0:T(512)} %get-tuple-element.34) | copy-start | bytes 3844
  231.1 80.5 %copy-start.7 = (f32[320]{0:T(512)S(1)}, f32[320]{0:T(512)}, u32[]{:S(2)}) copy-start(f32[320]{0:T(512)} %get-tuple-element.65) | copy-start | bytes 3844
  317.3 2.6 copy-start.2
  321.9 30.4 %copy-start.15 = (f32[320]{0:T(512)S(1)}, f32[320]{0:T(512)}, u32[]{:S(2)}) copy-start(f32[320]{0:T(512)} %get-tuple-element.38) | copy-start | bytes 3844
  324.0 18.3 %collective-permute-start.6 = (bf16[16,1,128,320]{2,3,1,0:T(8,128)(2,1)S(1)}, bf16[16,1,128,320]{2,3,1,0:T(8,128)(2,1)}, u32[]{:S(2)}, u32[]{:S(2)}) collective-permute-start(bf16[16,1,128,320]{2,3,1,0:T(8,128)(2,1)S(1)} %copy.71), channel_id=1, source_target_pairs={{0,1},{1,2},{2,3},{3,4},{4,5},{5,6},{6,7},{7,8},{8,9},{9,10},{10,1... | collective-permute-start | bytes 3932168 | tf_op jit(solution)/shard_map/ppermute | solution.py:38
  330.5 18.9 %collective-permute-start.7 = (bf16[16,1,128,320]{2,3,1,0:T(8,128)(2,1)}, bf16[16,1,128,320]{2,3,1,0:T(8,128)(2,1)}, u32[]{:S(2)}, u32[]{:S(2)}) collective-permute-start(bf16[16,1,128,320]{2,3,1,0:T(8,128)(2,1)} %copy.72), channel_id=1, source_target_pairs={{1,0},{2,1},{3,2},{4,3},{5,4},{6,5},{7,6},{8,7},{9,8},{10,9},{11,1... | collective-permute-start | bytes 3932168 | tf_op jit(solution)/shard_map/ppermute | solution.py:41
  352.3 79.7 %copy-start.8 = (f32[320]{0:T(512)S(1)}, f32[320]{0:T(512)}, u32[]{:S(2)}) copy-start(f32[320]{0:T(512)} %get-tuple-element.28) | copy-start | bytes 3844
  352.3 79.7 %copy-start.9 = (f32[320]{0:T(512)S(1)}, f32[320]{0:T(512)}, u32[]{:S(2)}) copy-start(f32[320]{0:T(512)} %get-tuple-element.67) | copy-start | bytes 3844
  438.0 2.6 copy-start.4
  444.6 18.3 %collective-permute-start.8 = (bf16[16,1,128,320]{2,3,1,0:T(8,128)(2,1)S(1)}, bf16[16,1,128,320]{2,3,1,0:T(8,128)(2,1)}, u32[]{:S(2)}, u32[]{:S(2)}) collective-permute-start(bf16[16,1,128,320]{2,3,1,0:T(8,128)(2,1)S(1)} %copy.75), channel_id=1, source_target_pairs={{0,1},{1,2},{2,3},{3,4},{4,5},{5,6},{6,7},{7,8},{8,9},{9,10},{10,1... | collective-permute-start | bytes 3932168 | tf_op jit(solution)/shard_map/ppermute | solution.py:38
  451.1 18.9 %collective-permute-start.9 = (bf16[16,1,128,320]{2,3,1,0:T(8,128)(2,1)}, bf16[16,1,128,320]{2,3,1,0:T(8,128)(2,1)}, u32[]{:S(2)}, u32[]{:S(2)}) collective-permute-start(bf16[16,1,128,320]{2,3,1,0:T(8,128)(2,1)} %copy.76), channel_id=1, source_target_pairs={{1,0},{2,1},{3,2},{4,3},{5,4},{6,5},{7,6},{8,7},{9,8},{10,9},{11,1... | collective-permute-start | bytes 3932168 | tf_op jit(solution)/shard_map/ppermute | solution.py:41
  472.9 37.7 %copy-start.16 = (bf16[320]{0:T(512)(128)(2,1)S(1)}, bf16[320]{0:T(512)(128)(2,1)}, u32[]{:S(2)}) copy-start(bf16[320]{0:T(512)(128)(2,1)} %param.31) | copy-start | bytes 1924
  502.4 2.6 copy-start.5
  508.4 27.7 %collective-permute-start.10 = (bf16[16,1,128,320]{2,3,1,0:T(8,128)(2,1)S(1)}, bf16[16,1,128,320]{2,3,1,0:T(8,128)(2,1)}, u32[]{:S(2)}, u32[]{:S(2)}) collective-permute-start(bf16[16,1,128,320]{2,3,1,0:T(8,128)(2,1)S(1)} %copy.79), channel_id=1, source_target_pairs={{0,1},{1,2},{2,3},{3,4},{4,5},{5,6},{6,7},{7,8},{8,9},{9,10},{10,1... | collective-permute-start | bytes 3932168 | tf_op jit(solution)/shard_map/ppermute | solution.py:38
where the time goes:
time: 558 us; the launch traced here: 550 us
  blocking collectives  189 us (34%)
  matrix products  143 us (26%)
  local copies, waits for them, and re-layouts  103 us (18%)
  waiting for transfers between devices  52.4 us (9%)
  starting transfers between devices  31.5 us (6%)
  other arithmetic  28.3 us (5%)
    conv_general_dilated x6, matrix products, conv_valid_rows(): lax.conv_general_dilated(inputs, kernel, (stride, stride), ((0, 0), (1, 1...  140 us
    psum x2, blocking collectives, band_program(): sums_all = lax.psum(group_sums(hidden_f32), 'sp')  95.5 us
    psum x2, blocking collectives, band_program(): sums_all = lax.psum(group_sums(mixed_in), 'sp')  93.8 us
    unnamed x39, local copies, waits for them, and re-layouts  41.4 us
    ppermute x6, waiting for transfers between devices, row_from_above(): return lax.ppermute(band_block[:, -1:], 'sp', to_next)  34 us
    convert_element_type x4, other arithmetic, norm_silu(): jax.nn.silu(values * scale_bc[:, None, None, :] + offset_bc[:, None, None...  23.2 us
    ppermute x6, starting transfers between devices, row_from_above(): return lax.ppermute(band_block[:, -1:], 'sp', to_next)  21.4 us
    slice x12, local copies, waits for them, and re-layouts, row_from_above(): return lax.ppermute(band_block[:, -1:], 'sp', to_next)  20.4 us
  transfers between devices with their start and end apart: 11, of which 9 were waited for; matrix products, arithmetic and copies ran while one was open for 10% of the time, Pallas kernels for 0%

commit v1 on v0

v1 whole, which is shorter than its diff:
```python
import functools

import jax
import jax.numpy as jnp
from jax import lax
from jax.experimental import pallas as pl
from jax.experimental.pallas import tpu as pltpu
from jax.sharding import PartitionSpec as P

GN_GROUPS = 32
GN_EPS = 1e-5
QUAD = 4
LATENT_PAD = 16
MESH_ID = pl.DeviceIdType.MESH
F32 = jnp.float32
BF16 = jnp.bfloat16

COL_BIN, COL_BDOWN = 0, 1
COL_G1, COL_S1, COL_B1, COL_G2, COL_S2, COL_B2 = 2, 4, 6, 8, 10, 12
N_COLS = 14


def band_kernel(
    n_sp, axis,
    lat_hbm, win_ref, w1_hbm, w2_hbm, wd_hbm, par_ref, emb_ref, sel_ref,
    h0_hbm, h1_hbm, h2_hbm, d_hbm,
    lat, xl, hb, ub, xb, w1, w2, wd, bc, stat, scl, ofs, inv_b, mean_b, sbuf, rbuf, dbuf,
    lat_sem, w_sem, out_sem, d_sem, latx_send, latx_recv, st_send, st_recv, u_send, u_recv, h_send, h_recv,
):
    n_quad, _, chan, lanes = hb.shape
    cols = lanes // QUAD
    group_ch = chan // GN_GROUPS
    kk = 3 * chan
    rows = h0_hbm.shape[1]
    chunk = 80
    me = lax.axis_index(axis)
    above = lax.rem(me + n_sp - 1, n_sp)
    below = lax.rem(me + 1, n_sp)
    has_above = me > 0
    has_below = me < n_sp - 1
    count = float(rows * n_sp * cols * group_ch)

    def peer(dist):
        return lax.rem(me + dist, n_sp)

    lat_load = pltpu.make_async_copy(lat_hbm, lat.at[:, 2 : 2 + rows], lat_sem)
    lat_load.start()
    w_loads = [
        pltpu.make_async_copy(w1_hbm.at[0], w1.at[0], w_sem.at[0]),
        pltpu.make_async_copy(w2_hbm.at[0], w2.at[0], w_sem.at[1]),
        pltpu.make_async_copy(w1_hbm.at[1], w1.at[1], w_sem.at[2]),
        pltpu.make_async_copy(w2_hbm.at[1], w2.at[1], w_sem.at[3]),
        pltpu.make_async_copy(wd_hbm, wd, w_sem.at[4]),
    ]
    for load in w_loads:
        load.start()

    barrier = pltpu.get_barrier_semaphore()

    @pl.loop(1, n_sp)
    def _(dist):
        pl.semaphore_signal(barrier, inc=1, device_id={axis: peer(dist)}, device_id_type=MESH_ID)

    pl.semaphore_wait(barrier, n_sp - 1)

    lat_down = pltpu.make_async_remote_copy(
        lat_hbm.at[:, rows - 2 : rows], lat.at[:, 0:2], latx_send.at[0], latx_recv.at[0], device_id={axis: below}, device_id_type=MESH_ID)
    lat_up = pltpu.make_async_remote_copy(
        lat_hbm.at[:, 0:2], lat.at[:, 2 + rows : 4 + rows], latx_send.at[1], latx_recv.at[1], device_id={axis: above}, device_id_type=MESH_ID)
    lat_down.start()
    lat_up.start()

    for col in range(N_COLS):
        bc[col] = jnp.broadcast_to(par_ref[:, col : col + 1], (chan, cols))

    lane_id = lax.broadcasted_iota(jnp.int32, (chunk, cols), 1)
    lane_id_small = lax.broadcasted_iota(jnp.int32, (LATENT_PAD, cols), 1)

    def store_taps(dst, base, stride, c0, size, k, val, ids):
        left = jnp.where(ids == 0, 0.0, pltpu.roll(val, 1, 1))
        right = jnp.where(ids == cols - 1, 0.0, pltpu.roll(val, cols - 1, 1))
        for tap, piece in enumerate((left, val, right)):
            dst[pl.ds(base + tap * stride + c0, size), k * cols : (k + 1) * cols] = piece.astype(BF16)

    def zero_stats():
        stat[...] = jnp.zeros_like(stat)

    def add_stats(k, c0, val):
        stat[k, pl.ds(c0, chunk), :] += val
        stat[QUAD + k, pl.ds(c0, chunk), :] += val * val

    def stats_copy(par, q, dist):
        return pltpu.make_async_remote_copy(
            sbuf.at[par, q], rbuf.at[par, q, dist - 1], st_send.at[par, q], st_recv.at[par, q],
            device_id={axis: peer(dist)}, device_id_type=MESH_ID)

    def send_stats(par, q):
        lane32 = lax.broadcasted_iota(jnp.int32, (GN_GROUPS, cols), 1)
        packed = jnp.zeros((GN_GROUPS, cols), F32)
        for idx in range(2 * QUAD):
            ref = stat.at[idx]
            group = ref[pl.ds(0, GN_GROUPS, stride=group_ch), :]
            for j in range(1, group_ch):
                group = group + ref[pl.ds(j, GN_GROUPS, stride=group_ch), :]
            packed = jnp.where(lane32 == idx, jnp.sum(group, axis=1, keepdims=True), packed)
        square = jnp.concatenate([packed, jnp.zeros((cols - GN_GROUPS, cols), F32)], axis=0)
        sbuf[par, q] = jnp.transpose(square)[: 2 * QUAD, :]

        @pl.loop(1, n_sp)
        def _(dist):
            stats_copy(par, q, dist).start()

    def wait_stats(par, q):
        whole = pltpu.make_async_remote_copy(
            rbuf.at[par, q], rbuf.at[par, q], st_send.at[par, q], st_recv.at[par, q],
            device_id={axis: below}, device_id_type=MESH_ID)
        whole.wait_send()
        whole.wait_recv()

    def make_scale(par, q, col_g, col_s, emb_idx):
        total = sbuf[par, q]
        for d in range(n_sp - 1):
            total = total + rbuf[par, q, d]
        mean = total[:QUAD] / count
        var = total[QUAD:] / count - mean * mean
        inv = lax.rsqrt(var + GN_EPS)
        square = jnp.concatenate([mean, inv, jnp.zeros((cols - 2 * QUAD, cols), F32)], axis=0)
        flipped = jnp.transpose(square)[:GN_GROUPS, :]
        for k in range(QUAD):
            mean_k = jnp.broadcast_to(flipped[:, k : k + 1], (GN_GROUPS, cols))
            inv_k = jnp.broadcast_to(flipped[:, QUAD + k : QUAD + k + 1], (GN_GROUPS, cols))
            for j in range(group_ch):
                mean_b.at[k][pl.ds(j, GN_GROUPS, stride=group_ch), :] = mean_k
                inv_b.at[k][pl.ds(j, GN_GROUPS, stride=group_ch), :] = inv_k
        for k in range(QUAD):
            for c0 in range(0, chan, chunk):
                cs = pl.ds(c0, chunk)
                half_scale = inv_b[k, cs, :] * (0.5 * bc[col_g, cs, :])
                center = mean_b[k, cs, :]
                if emb_idx is not None:
                    center = center - emb_ref[emb_idx, cs, k : k + 1]
                scl[k, cs, :] = half_scale
                ofs[k, cs, :] = 0.5 * bc[col_s, cs, :] - center * half_scale

    def norm_rows(src, q):
        @pl.loop(0, rows + 2)
        def _(row):
            keep = jnp.logical_and(jnp.logical_or(row > 0, has_above), jnp.logical_or(row < rows + 1, has_below))
            flag = keep.astype(jnp.int32)
            for k in range(QUAD):
                for c0 in range(0, chan, chunk):
                    val = src[q, row, pl.ds(c0, chunk), k * cols : (k + 1) * cols].astype(F32)
                    half = val * scl[k, pl.ds(c0, chunk), :] + ofs[k, pl.ds(c0, chunk), :]
                    half = jnp.where(flag > 0, half, 0.0)
                    act = half + half * jnp.tanh(half)
                    store_taps(xb, row * kk, chan, c0, chunk, k, act, lane_id)

    def halo_copies(buf, send, recv, q):
        down = pltpu.make_async_remote_copy(
            buf.at[q, rows], buf.at[q, 0], send.at[q, 0], recv.at[q, 0], device_id={axis: below}, device_id_type=MESH_ID)
        up = pltpu.make_async_remote_copy(
            buf.at[q, 1], buf.at[q, rows + 1], send.at[q, 1], recv.at[q, 1], device_id={axis: above}, device_id_type=MESH_ID)
        return down, up

    def send_halo(buf, send, recv, q):
        for copy in halo_copies(buf, send, recv, q):
            copy.start()

    def wait_halo(buf, send, recv, q):
        for copy in halo_copies(buf, send, recv, q):
            copy.wait()

    def out_copies(dst, q):
        return [
            pltpu.make_async_copy(hb.at[q, 1 : 1 + rows, :, k * cols : (k + 1) * cols], dst.at[q * QUAD + k], out_sem.at[q, k])
            for k in range(QUAD)
        ]

    lat_load.wait()
    lat_down.wait()
    lat_up.wait()

    @pl.loop(0, n_quad)
    def _(q):
        for row in range(rows + 4):
            for k in range(QUAD):
                val = lat[q, row, :, k * cols : (k + 1) * cols].astype(F32)
                if row < 2:
                    val = jnp.where(has_above, val, 0.0)
                if row >= rows + 2:
                    val = jnp.where(has_below, val, 0.0)
                store_taps(xl, row * 3 * LATENT_PAD, LATENT_PAD, 0, LATENT_PAD, k, val, lane_id_small)
        zero_stats()
        for row in range(rows + 2):
            acc = jnp.dot(win_ref[...], xl[row * 3 * LATENT_PAD : (row + 3) * 3 * LATENT_PAD, :], preferred_element_type=F32)
            for k in range(QUAD):
                for c0 in range(0, chan, chunk):
                    val = (acc[c0 : c0 + chunk, k * cols : (k + 1) * cols] + bc[COL_BIN, c0 : c0 + chunk, :]).astype(BF16)
                    hb[q, row, c0 : c0 + chunk, k * cols : (k + 1) * cols] = val
                    if 1 <= row <= rows:
                        add_stats(k, c0, val.astype(F32))
        send_stats(0, q)
        for copy in out_copies(h0_hbm, q):
            copy.start()

    @pl.loop(0, w1.shape[0])
    def _(layer):
        for idx in range(w1.shape[0]):
            @pl.when(layer == idx)
            def _():
                w_loads[2 * idx].wait()

        @pl.loop(0, n_quad)
        def _(q):
            wait_stats(0, q)

            @pl.when(layer > 0)
            def _():
                wait_halo(hb, h_send, h_recv, q)

            make_scale(0, q, COL_G1 + layer, COL_S1 + layer, None)
            norm_rows(hb, q)
            zero_stats()

            @pl.loop(0, rows)
            def _(row):
                acc = jnp.dot(w1[layer], xb[pl.ds(row * kk, 3 * kk), :], preferred_element_type=F32)
                for k in range(QUAD):
                    for c0 in range(0, chan, chunk):
                        cs = pl.ds(c0, chunk)
                        val = (acc[c0 : c0 + chunk, k * cols : (k + 1) * cols] + bc[COL_B1 + layer, cs, :]).astype(BF16)
                        ub[q, row + 1, cs, k * cols : (k + 1) * cols] = val
                        add_stats(k, c0, val.astype(F32) + emb_ref[layer * n_quad + q, cs, k : k + 1])

            send_halo(ub, u_send, u_recv, q)
            send_stats(1, q)

        for idx in range(w1.shape[0]):
            @pl.when(layer == idx)
            def _():
                w_loads[2 * idx + 1].wait()

        @pl.loop(0, n_quad)
        def _(q):
            wait_stats(1, q)
            wait_halo(ub, u_send, u_recv, q)
            make_scale(1, q, COL_G2 + layer, COL_S2 + layer, layer * n_quad + q)
            norm_rows(ub, q)
            zero_stats()
            for copy in out_copies(h0_hbm, q):
                copy.wait()

            @pl.loop(0, rows)
            def _(row):
                acc = jnp.dot(w2[layer], xb[pl.ds(row * kk, 3 * kk), :], preferred_element_type=F32)
                for k in range(QUAD):
                    for c0 in range(0, chan, chunk):
                        cs = pl.ds(c0, chunk)
                        branch = (acc[c0 : c0 + chunk, k * cols : (k + 1) * cols] + bc[COL_B2 + layer, cs, :]).astype(BF16).astype(F32)
                        val = (hb[q, row + 1, cs, k * cols : (k + 1) * cols].astype(F32) + branch).astype(BF16)
                        hb[q, row + 1, cs, k * cols : (k + 1) * cols] = val
                        add_stats(k, c0, val.astype(F32))

            send_halo(hb, h_send, h_recv, q)

            @pl.when(layer == 0)
            def _():
                send_stats(0, q)
                for copy in out_copies(h1_hbm, q):
                    copy.start()

            @pl.when(layer > 0)
            def _():
                for copy in out_copies(h2_hbm, q):
                    copy.start()

    w_loads[4].wait()

    def d_copies(q):
        return [pltpu.make_async_copy(dbuf.at[q, k], d_hbm.at[q * QUAD + k], d_sem.at[q, k]) for k in range(QUAD)]

    @pl.loop(0, n_quad)
    def _(q):
        wait_halo(hb, h_send, h_recv, q)

        @pl.loop(0, rows + 1)
        def _(row):
            keep = jnp.logical_or(row > 0, has_above)
            flag = keep.astype(jnp.int32)
            for k in range(QUAD):
                for c0 in range(0, chan, chunk):
                    val = hb[q, row, pl.ds(c0, chunk), k * cols : (k + 1) * cols].astype(F32)
                    val = jnp.where(flag > 0, val, 0.0)
                    store_taps(xb, row * kk, chan, c0, chunk, k, val, lane_id)

        @pl.loop(0, rows // 2)
        def _(row):
            acc = jnp.dot(wd[...], xb[pl.ds(2 * row * kk, 3 * kk), :], preferred_element_type=F32)
            for k in range(QUAD):
                full = (acc[:, k * cols : (k + 1) * cols] + bc[COL_BDOWN]).astype(BF16)
                picked = lax.dot_general(sel_ref[...], full, (((1,), (1,)), ((), ())), preferred_element_type=F32)
                dbuf[q, k, row] = picked.astype(BF16)

        for copy in d_copies(q):
            copy.start()

    @pl.loop(0, n_quad)
    def _(q):
        for copy in out_copies(h2_hbm, q):
            copy.wait()
        for copy in d_copies(q):
            copy.wait()


def solution(mesh):
    n_sp = mesh.shape["sp"]

    def band_program(latent, time_emb, w_in, b_in, gn1_scale, gn1_shift, conv1_w, conv1_b, temb_w, temb_b, gn2_scale, gn2_shift, conv2_w, conv2_b, down_w, down_b):
        batch, rows, cols, lat_ch = latent.shape
        chan = w_in.shape[-1]
        layers = conv1_w.shape[0]
        n_quad = batch // QUAD
        lanes = QUAD * cols
        kk = 3 * chan

        lat = latent.reshape(n_quad, QUAD, rows, cols, lat_ch).transpose(0, 2, 4, 1, 3).reshape(n_quad, rows, lat_ch, lanes)
        lat = jnp.pad(lat, ((0, 0), (0, 0), (0, LATENT_PAD - lat_ch), (0, 0)))
        win = jnp.pad(w_in, ((0, 0), (0, 0), (0, LATENT_PAD - lat_ch), (0, 0))).reshape(9 * LATENT_PAD, chan).T
        w1 = conv1_w.reshape(layers, 9 * chan, chan).transpose(0, 2, 1)
        w2 = conv2_w.reshape(layers, 9 * chan, chan).transpose(0, 2, 1)
        wd = down_w.reshape(9 * chan, chan).T
        par = jnp.concatenate([b_in[None], down_b[None], gn1_scale, gn1_shift, conv1_b, gn2_scale, gn2_shift, conv2_b], axis=0).astype(F32).T
        emb_act = jax.nn.silu(time_emb.astype(F32)).astype(BF16)
        emb = jnp.einsum("bt,ltc->lbc", emb_act, temb_w, preferred_element_type=F32) + temb_b.astype(F32)[:, None, :]
        emb = emb.reshape(layers * n_quad, QUAD, chan).transpose(0, 2, 1)
        sel = (lax.broadcasted_iota(jnp.int32, (cols // 2, cols), 1) == 2 * lax.broadcasted_iota(jnp.int32, (cols // 2, cols), 0)).astype(BF16)

        band = jax.ShapeDtypeStruct((batch, rows, chan, cols), BF16)
        hbm = pl.BlockSpec(memory_space=pl.ANY)
        vmem = pl.BlockSpec(memory_space=pltpu.VMEM)
        dma = pltpu.SemaphoreType.DMA
        h0, h1, h2, d = pl.pallas_call(
            functools.partial(band_kernel, n_sp, "sp"),
            out_shape=(band, band, band, jax.ShapeDtypeStruct((batch, rows // 2, cols // 2, chan), BF16)),
            in_specs=[hbm, vmem, hbm, hbm, hbm, vmem, vmem, vmem],
            out_specs=(hbm,) * 4,
            scratch_shapes=[
                pltpu.VMEM((n_quad, rows + 4, LATENT_PAD, lanes), BF16),
                pltpu.VMEM(((rows + 4) * 3 * LATENT_PAD, lanes), BF16),
                pltpu.VMEM((n_quad, rows + 2, chan, lanes), BF16),
                pltpu.VMEM((n_quad, rows + 2, chan, lanes), BF16),
                pltpu.VMEM(((rows + 2) * kk, lanes), BF16),
                pltpu.VMEM((layers, chan, 9 * chan), BF16),
                pltpu.VMEM((layers, chan, 9 * chan), BF16),
                pltpu.VMEM((chan, 9 * chan), BF16),
                pltpu.VMEM((N_COLS, chan, cols), F32),
                pltpu.VMEM((2 * QUAD, chan, cols), F32),
                pltpu.VMEM((QUAD, chan, cols), F32),
                pltpu.VMEM((QUAD, chan, cols), F32),
                pltpu.VMEM((QUAD, chan, cols), F32),
                pltpu.VMEM((QUAD, chan, cols), F32),
                pltpu.VMEM((2, n_quad, 2 * QUAD, cols), F32),
                pltpu.VMEM((2, n_quad, n_sp - 1, 2 * QUAD, cols), F32),
                pltpu.VMEM((n_quad, QUAD, rows // 2, cols // 2, chan), BF16),
                dma, dma((5,)), dma((n_quad, QUAD)), dma((n_quad, QUAD)),
                dma((2,)), dma((2,)), dma((2, n_quad)), dma((2, n_quad)),
                dma((n_quad, 2)), dma((n_quad, 2)), dma((n_quad, 2)), dma((n_quad, 2)),
            ],
            compiler_params=pltpu.CompilerParams(collective_id=0, has_side_effects=True, vmem_limit_bytes=60 * 1024 * 1024),
            name="band",
        )(lat, win, w1, w2, wd, par, emb, sel)
        return tuple(h.transpose(0, 1, 3, 2) for h in (h0, h1, h2)) + (d,)

    band_spec = P("dp", "sp", None, None)
    return jax.shard_map(band_program, mesh=mesh, in_specs=(band_spec, P("dp", None)) + (P(),) * 14, out_specs=(band_spec,) * 4, check_vma=False)
```

time: 558 us -> 220 us (0.39); the launches traced: 550 us -> 219 us
  blocking collectives: 189 us -> 0 us
  Pallas kernels: 0 us -> 178 us
  matrix products: 143 us -> 1.34 us
  local copies, waits for them, and re-layouts: 103 us -> 38 us
  waiting for transfers between devices: 52.4 us -> 0 us
  starting transfers between devices: 31.5 us -> 0 us
  other arithmetic: 28.3 us -> 1.36 us
    psum x4 -> x0, blocking collectives: 189 us -> none  [the longest x2 95.5 us: band_program(): sums_all = lax.psum(group_sums(hidden_f32), 'sp')]
    pallas_call x0 -> x1, Pallas kernels: none -> 178 us  [band_program(): pl.pallas_call(functools.partial(band_kernel, n_sp, 'sp'), out_shape=(ban...]
    conv_general_dilated x6 -> x0, matrix products: 140 us -> none  [conv_valid_rows(): lax.conv_general_dilated(inputs, kernel, (stride, stride), ((0, 0), (1, 1...]
    ppermute x11 -> x0, waiting for transfers between devices: 52.4 us -> none  [the longest x6 34 us: row_from_above(): return lax.ppermute(band_block[:, -1:], 'sp', to_next)]
    slice x17 -> x0, local copies, waits for them, and re-layouts: 31.6 us -> none  [the longest x12 20.4 us: row_from_above(): return lax.ppermute(band_block[:, -1:], 'sp', to_next)]
    ppermute x11 -> x0, starting transfers between devices: 31.5 us -> none  [the longest x6 21.4 us: row_from_above(): return lax.ppermute(band_block[:, -1:], 'sp', to_next)]
    unnamed x39 -> x14, local copies, waits for them, and re-layouts: 41.4 us -> 13 us
    ppermute x9 -> x0, local copies, waits for them, and re-layouts: 25.7 us -> none  [the longest x5 14.3 us: row_from_above(): return lax.ppermute(band_block[:, -1:], 'sp', to_next)]
  transfers between devices with their start and end apart: 11 -> 0, of which waited for: 9 -> 0; matrix products, arithmetic and copies ran while one was open for 10% -> 0% of each run, Pallas kernels for 0% -> 0%
where the time goes in v1:
time: 220 us; the launch traced here: 219 us
  Pallas kernels  178 us (81%)
  local copies, waits for them, and re-layouts  38 us (17%)
    pallas_call x1, Pallas kernels, band_program(): pl.pallas_call(functools.partial(band_kernel, n_sp, 'sp'), out_shape=(ban...  178 us
    unnamed x14, local copies, waits for them, and re-layouts  13 us
    reshape x1, local copies, waits for them, and re-layouts, band_program(): w1 = conv1_w.reshape(layers, 9 * chan, chan).transpose(0, 2, 1)  6.23 us
    reshape x1, local copies, waits for them, and re-layouts, band_program(): w2 = conv2_w.reshape(layers, 9 * chan, chan).transpose(0, 2, 1)  6.23 us

profile of v1, /device:TPU:97, one launch (start us, length us, event | category | flops | bytes accessed | tf_op | source)
XLA Modules:
  0.0 218.9 jit_solution(8265650623657090965)
XLA Ops:
  0.6 0.0 copy-start
  0.7 0.8 broadcast_in_dim.7
  1.5 0.7 broadcast_in_dim.8
  2.1 0.7 convert_element_type.19
  2.8 1.5 concatenate.3
  4.3 0.7 fusion.8.sel_ref
  5.0 0.0 copy-done
  5.0 1.3 fusion
  6.4 0.9 copy.53
  7.3 0.8 pad.9
  8.1 0.8 copy.46
  8.8 0.8 copy.50
  9.6 0.7 pad.8.lat_hbm
  10.4 1.5 copy.51
  11.9 4.0 %copy.49 = bf16[2880,320]{0,1:T(8,128)(2,1)} copy(bf16[2880,320]{1,0:T(8,128)(2,1)} %bitcast.34) | data formatting | bytes 3686400 | tf_op jit(solution)/shard_map/reshape | solution.py:331
  15.9 6.2 %copy.47 = bf16[2,2880,320]{1,2,0:T(8,128)(2,1)} copy(bf16[2,2880,320]{2,1,0:T(8,128)(2,1)} %bitcast.32) | data formatting | bytes 7372800 | tf_op jit(solution)/shard_map/reshape | solution.py:329
  22.1 6.2 %copy.48 = bf16[2,2880,320]{1,2,0:T(8,128)(2,1)} copy(bf16[2,2880,320]{2,1,0:T(8,128)(2,1)} %bitcast.33) | data formatting | bytes 7372800 | tf_op jit(solution)/shard_map/reshape | solution.py:330
  28.4 177.5 %band.1 = (bf16[16,4,320,128]{3,2,1,0:T(8,128)(2,1)}, bf16[16,4,320,128]{3,2,1,0:T(8,128)(2,1)}, bf16[16,4,320,128]{3,2,1,0:T(8,128)(2,1)}, bf16[16,2,64,320]{3,2,1,0:T(8,128)(2,1)}) custom-call(bf16[4,4,16,512]{3,2,1,0:T(8,128)(2,1)} %pad.8.lat_hbm, bf16[320,144]{1,0:T(8,128)(2,1)} %bitcast.36, bf16[2,320,2880]{2,1,0:T(8,128)(2,1)} %bitcast.23, ...), custom_call_target="tpu_custom_call" | custom-call | tf_op jit(solution)/shard_map/band/pallas_call | solution.py:342
  205.9 0.0 copy-start.1
  205.9 0.0 slice-start
  205.9 5.8 %copy.58 = bf16[16,4,128,320]{2,3,1,0:T(8,128)(2,1)} copy(bf16[16,4,128,320]{2,3,1,0:T(8,128)(2,1)} %bitcast.30) | data formatting | bytes 10485760
  211.7 0.0 copy-done.1
  211.7 0.0 slice-start.1
  211.7 2.6 %copy.59 = bf16[16,4,128,320]{2,3,1,0:T(8,128)(2,1)} copy(bf16[16,4,128,320]{2,3,1,0:T(8,128)(2,1)S(1)} %bitcast.29) | data formatting | bytes 10485760
  214.3 0.0 slice-done
  214.3 1.0 slice-done.1
  215.3 0.0 copy-start.2
  215.3 2.4 %copy.60 = bf16[16,4,128,320]{2,3,1,0:T(8,128)(2,1)} copy(bf16[16,4,128,320]{2,3,1,0:T(8,128)(2,1)S(1)} %bitcast.28) | data formatting | bytes 10485760
  217.6 0.2 copy-done.2
  217.8 1.1 copy.61
  (4 shorter events, 0.1 us)
Async XLA Ops:
  0.6 4.4 %copy-start = (bf16[2,1280,320]{1,2,0:T(8,128)(2,1)S(1)}, bf16[2,1280,320]{1,2,0:T(8,128)(2,1)}, u32[]{:S(2)}) copy-start(bf16[2,1280,320]{1,2,0:T(8,128)(2,1)} %param.24) | copy-start | bytes 4915204
  205.9 5.8 %copy-start.1 = (bf16[16,4,320,128]{3,2,1,0:T(8,128)(2,1)S(1)}, bf16[16,4,320,128]{3,2,1,0:T(8,128)(2,1)}, u32[]{:S(2)}) copy-start(bf16[16,4,320,128]{3,2,1,0:T(8,128)(2,1)} %get-tuple-element.9) | copy-start | bytes 15728644
  205.9 8.4 %slice-start = ((s8[5242880]{0:T(1024)(128)(4,1)}), s8[4194304]{0:T(1024)(128)(4,1)S(1)}, s32[]{:S(2)}) async-start(s8[5242880]{0:T(1024)(128)(4,1)} %bitcast.26), calls=%async_computation | async-start | bytes 8388608
  211.7 3.6 %slice-start.1 = ((s8[5242880]{0:T(1024)(128)(4,1)}), s8[1048576]{0:T(1024)(128)(4,1)S(1)}, s32[]{:S(2)}) async-start(s8[5242880]{0:T(1024)(128)(4,1)} %bitcast.26), calls=%async_computation.1 | async-start | bytes 2097152
  215.3 2.5 %copy-start.2 = (bf16[16,2,64,320]{3,2,1,0:T(8,128)(2,1)S(1)}, bf16[16,2,64,320]{3,2,1,0:T(8,128)(2,1)}, u32[]{:S(2)}) copy-start(bf16[16,2,64,320]{3,2,1,0:T(8,128)(2,1)} %get-tuple-element.19) | copy-start | bytes 3932164

commit v2 on v1

v2 whole, which is shorter than its diff:
```python
import functools

import jax
import jax.numpy as jnp
from jax import lax
from jax.experimental import pallas as pl
from jax.experimental.pallas import tpu as pltpu
from jax.sharding import PartitionSpec as P

GN_GROUPS = 32
GN_EPS = 1e-5
QUAD = 4
LATENT_PAD = 16
CORES = 2
MESH_ID = pl.DeviceIdType.MESH
F32 = jnp.float32
BF16 = jnp.bfloat16

COL_BIN = 0
COL_G1, COL_S1, COL_B1, COL_G2, COL_S2, COL_B2 = 1, 3, 5, 7, 9, 11
COL_BDOWN = 13
N_COLS = 13


def store_shifts(dst, base, stride, k, val):
    size, cols = val.shape
    lane = lax.broadcasted_iota(jnp.int32, val.shape, 1)
    zero = jnp.zeros_like(val)
    left = jnp.where(lane == 0, zero, pltpu.roll(val, 1, 1))
    right = jnp.where(lane == cols - 1, zero, pltpu.roll(val, cols - 1, 1))
    for tap, piece in enumerate((left, val, right)):
        dst[base + tap * stride : base + tap * stride + size, k * cols : (k + 1) * cols] = piece


def transpose_weight(raw, out):
    for start in range(0, out.shape[1], 128):
        out[:, start : start + 128] = jnp.transpose(raw[start : start + 128, :])


def band_kernel(
    n_sp, axis,
    lat_hbm, win_ref, w1_hbm, w2_hbm, wd_hbm, par_ref, emb_ref,
    h0_hbm, h1_hbm, h2_hbm, halo_hbm, wt_hbm,
    lat, xl, act, xb0, xb1, raw, wt, acc_a, acc_b, bc, stat_a, stat_b, scl, ofs, inv_b, mean_b, sbuf_a, rbuf_a, sbuf, rbuf,
    lat_sem, w_sem, wt_sem, out_sem, d_sem, latx_send, latx_recv, sa_send, sa_recv, st_send, st_recv, x_send, x_recv,
):
    _, n_quad, _, chan, lanes = act.shape
    cols = lanes // QUAD
    group_ch = chan // GN_GROUPS
    kk = 3 * chan
    rows = h0_hbm.shape[1]
    chunk = 80
    me = lax.axis_index(axis)
    above = lax.rem(me + n_sp - 1, n_sp)
    below = lax.rem(me + 1, n_sp)
    partner = me + 1 - 2 * lax.rem(me, 2)
    n_far = n_sp // CORES - 1
    has_above = me > 0
    has_below = me < n_sp - 1
    count = float(rows * n_sp * cols * group_ch)

    def peer(dist):
        return lax.rem(me + dist, n_sp)

    lat_load = pltpu.make_async_copy(lat_hbm, lat.at[:, 2 : 2 + rows], lat_sem)
    lat_load.start()

    def w_load(idx):
        src = wd_hbm if idx == 2 * w1_hbm.shape[0] else (w1_hbm, w2_hbm)[idx % 2].at[idx // 2]
        return pltpu.make_async_copy(src, raw.at[idx % 2, : 3 * kk], w_sem.at[idx % 2])

    w_load(0).start()
    w_load(1).start()

    barrier = pltpu.get_barrier_semaphore()

    @pl.loop(1, n_sp)
    def _(dist):
        pl.semaphore_signal(barrier, inc=1, device_id={axis: peer(dist)}, device_id_type=MESH_ID)

    pl.semaphore_wait(barrier, n_sp - 1)

    lat_down = pltpu.make_async_remote_copy(
        lat_hbm.at[:, rows - 2 : rows], lat.at[:, 0:2], latx_send.at[0], latx_recv.at[0], device_id={axis: below}, device_id_type=MESH_ID)
    lat_up = pltpu.make_async_remote_copy(
        lat_hbm.at[:, 0:2], lat.at[:, 2 + rows : 4 + rows], latx_send.at[1], latx_recv.at[1], device_id={axis: above}, device_id_type=MESH_ID)
    lat_down.start()
    lat_up.start()

    for col in range(N_COLS):
        bc[col] = jnp.broadcast_to(par_ref[:, col : col + 1], (chan, cols))

    lane_id_small = lax.broadcasted_iota(jnp.int32, (LATENT_PAD, cols), 1)

    def store_taps(dst, base, k, val):
        left = jnp.where(lane_id_small == 0, 0.0, pltpu.roll(val, 1, 1))
        right = jnp.where(lane_id_small == cols - 1, 0.0, pltpu.roll(val, cols - 1, 1))
        for tap, piece in enumerate((left, val, right)):
            dst[pl.ds(base + tap * LATENT_PAD, LATENT_PAD), k * cols : (k + 1) * cols] = piece.astype(BF16)

    def add_stats(acc_ref, first, k, c0, val):
        cs = pl.ds(c0, chunk)
        if first:
            acc_ref[k, cs, :] = val
            acc_ref[QUAD + k, cs, :] = val * val
        else:
            acc_ref[k, cs, :] += val
            acc_ref[QUAD + k, cs, :] += val * val

    def pack_stats(acc_ref, par, q):
        lane32 = lax.broadcasted_iota(jnp.int32, (GN_GROUPS, cols), 1)
        packed = jnp.zeros((GN_GROUPS, cols), F32)
        for idx in range(2 * QUAD):
            ref = acc_ref.at[idx]
            group = ref[pl.ds(0, GN_GROUPS, stride=group_ch), :]
            for j in range(1, group_ch):
                group = group + ref[pl.ds(j, GN_GROUPS, stride=group_ch), :]
            packed = jnp.where(lane32 == idx, jnp.sum(group, axis=1, keepdims=True), packed)
        square = jnp.concatenate([packed, jnp.zeros((cols - GN_GROUPS, cols), F32)], axis=0)
        sbuf_a[par, q] = jnp.transpose(square)[: 2 * QUAD, :]

    def pair_copy(par, q):
        return pltpu.make_async_remote_copy(
            sbuf_a.at[par, q], rbuf_a.at[par, q], sa_send.at[par, q], sa_recv.at[par, q],
            device_id={axis: partner}, device_id_type=MESH_ID)

    def add_pair(par, q):
        sbuf[par, q] = sbuf_a[par, q] + rbuf_a[par, q]

    def send_stats(par, q, first=1, last=None):
        for dist in range(first, n_far + 1 if last is None else last):
            pltpu.make_async_remote_copy(
                sbuf.at[par, q], rbuf.at[par, q, dist - 1], st_send.at[par, q], st_recv.at[par, q],
                device_id={axis: peer(CORES * dist)}, device_id_type=MESH_ID).start()

    def wait_stats(par, q):
        pair_copy(par, q).wait_send()
        whole = pltpu.make_async_remote_copy(
            rbuf.at[par, q], rbuf.at[par, q], st_send.at[par, q], st_recv.at[par, q],
            device_id={axis: below}, device_id_type=MESH_ID)
        whole.wait_send()
        whole.wait_recv()

    def make_scale(par, q, col_g, col_s, emb_idx, use_emb):
        parts = [sbuf[par, q]] + [rbuf[par, q, d] for d in range(n_far)]
        while len(parts) > 1:
            parts = [parts[i] + parts[i + 1] for i in range(0, len(parts) - 1, 2)] + ([parts[-1]] if len(parts) % 2 else [])
        total = parts[0]
        mean = total[:QUAD] / count
        var = total[QUAD:] / count - mean * mean
        inv = lax.rsqrt(var + GN_EPS)
        square = jnp.concatenate([mean, inv, jnp.zeros((cols - 2 * QUAD, cols), F32)], axis=0)
        flipped = jnp.transpose(square)[:GN_GROUPS, :]
        for k in range(QUAD):
            mean_k = jnp.broadcast_to(flipped[:, k : k + 1], (GN_GROUPS, cols))
            inv_k = jnp.broadcast_to(flipped[:, QUAD + k : QUAD + k + 1], (GN_GROUPS, cols))
            for j in range(group_ch):
                mean_b.at[k][pl.ds(j, GN_GROUPS, stride=group_ch), :] = mean_k
                inv_b.at[k][pl.ds(j, GN_GROUPS, stride=group_ch), :] = inv_k
        for k in range(QUAD):
            for c0 in range(0, chan, chunk):
                cs = pl.ds(c0, chunk)
                half_scale = inv_b[k, cs, :] * (0.5 * bc[col_g, cs, :])
                center = mean_b[k, cs, :] - jnp.where(use_emb, emb_ref[emb_idx, cs, k : k + 1], 0.0)
                scl[k, cs, :] = half_scale
                ofs[k, cs, :] = 0.5 * bc[col_s, cs, :] - center * half_scale

    def norm_row(src, q, row, dst):
        for k in range(QUAD):
            for c0 in range(0, chan, chunk):
                val = act[src, q, row, pl.ds(c0, chunk), k * cols : (k + 1) * cols].astype(F32)
                half = val * scl[k, pl.ds(c0, chunk), :] + ofs[k, pl.ds(c0, chunk), :]
                if row == 0:
                    half = jnp.where(has_above, half, 0.0)
                if row == rows + 1:
                    half = jnp.where(has_below, half, 0.0)
                store_shifts(dst, row * kk + c0, chan, k, (half + half * jnp.tanh(half)).astype(BF16))

    def halo_copies(src, q):
        down = pltpu.make_async_remote_copy(
            act.at[src, q, rows], act.at[src, q, 0], x_send.at[src, q, 0], x_recv.at[src, q, 0], device_id={axis: below}, device_id_type=MESH_ID)
        up = pltpu.make_async_remote_copy(
            act.at[src, q, 1], act.at[src, q, rows + 1], x_send.at[src, q, 1], x_recv.at[src, q, 1], device_id={axis: above}, device_id_type=MESH_ID)
        return down, up

    def send_halo(src, q):
        for copy in halo_copies(src, q):
            copy.start()

    def wait_halo(src, q):
        for copy in halo_copies(src, q):
            copy.wait()

    def out_copies(dst, q):
        return [
            pltpu.make_async_copy(act.at[0, q, 1 : 1 + rows, :, k * cols : (k + 1) * cols], dst.at[q * QUAD + k], out_sem.at[q, k])
            for k in range(QUAD)
        ]

    lat_load.wait()
    lat_down.wait()
    lat_up.wait()

    @pl.loop(0, n_quad)
    def _(q):
        @pl.when(q > 0)
        def _():
            pack_stats(stat_b, 0, q - 1)
            pair_copy(0, q - 1).start()

        for row in range(rows + 4):
            for k in range(QUAD):
                val = lat[q, row, :, k * cols : (k + 1) * cols].astype(F32)
                if row < 2:
                    val = jnp.where(has_above, val, 0.0)
                if row >= rows + 2:
                    val = jnp.where(has_below, val, 0.0)
                store_taps(xl, row * 3 * LATENT_PAD, k, val)
        for row in range(rows + 2):
            if row == 3:
                @pl.when(q > 0)
                def _():
                    pair_copy(0, q - 1).wait_recv()
                    add_pair(0, q - 1)
                    send_stats(0, q - 1)

            acc = jnp.dot(win_ref[...], xl[row * 3 * LATENT_PAD : (row + 3) * 3 * LATENT_PAD, :], preferred_element_type=F32)
            for k in range(QUAD):
                for c0 in range(0, chan, chunk):
                    val = (acc[c0 : c0 + chunk, k * cols : (k + 1) * cols] + bc[COL_BIN, c0 : c0 + chunk, :]).astype(BF16)
                    act[0, q, row, c0 : c0 + chunk, k * cols : (k + 1) * cols] = val
                    if 1 <= row <= rows:
                        add_stats(stat_b, row == 1, k, c0, val.astype(F32))
        for copy in out_copies(h0_hbm, q):
            copy.start()

    pack_stats(stat_b, 0, n_quad - 1)
    pair_copy(0, n_quad - 1).start()

    n_conv = 2 * w1_hbm.shape[0]
    n_step = n_conv * n_quad
    xbs = (xb0, xb1)
    stats = (stat_a, stat_b)
    accs = (acc_a, acc_b)
    order = (0, rows - 1) + tuple(range(1, rows - 1))

    pair_copy(0, n_quad - 1).wait_recv()
    add_pair(0, n_quad - 1)
    send_stats(0, n_quad - 1)
    wait_stats(0, 0)
    make_scale(0, 0, COL_G1, COL_S1, 0, False)
    for row in range(rows + 2):
        norm_row(0, 0, row, xb0)

    def finish(step, pos, stat):
        phase, q = step // n_quad, step % n_quad
        conv, layer = phase % 2, phase // 2
        bcol = layer + (COL_B2 - COL_B1) * conv + COL_B1
        emb = layer * n_quad + q
        row, acc = order[pos], accs[pos % 2]
        for k in range(QUAD):
            ks = slice(k * cols, (k + 1) * cols)
            for c0 in range(0, chan, chunk):
                cs = pl.ds(c0, chunk)
                val = (acc[cs, ks] + bc[bcol, cs, :]).astype(BF16).astype(F32)
                val = (jnp.where(conv == 1, act[0, q, row + 1, cs, ks].astype(F32), 0.0) + val).astype(BF16)
                act[1 - conv, q, row + 1, cs, ks] = val
                add_stats(stat, pos == 0, k, c0, val.astype(F32) + jnp.where(conv == 0, emb_ref[emb, cs, k : k + 1], 0.0))

    def start_outputs(step):
        for idx, dst in enumerate((h1_hbm, h2_hbm)):
            @pl.when(step // n_quad == 2 * idx + 1)
            def _():
                for copy in out_copies(dst, step % n_quad):
                    copy.start()

    def slot(step, side):
        phase, q = step // n_quad, step % n_quad
        conv = phase % 2
        nphase, nq = (step + 1) // n_quad, (step + 1) % n_quad
        nconv, nlayer = nphase % 2, jnp.minimum(nphase // 2, n_conv // 2 - 1)
        prev = jnp.maximum(step - 1, 0)
        pphase, pq = prev // n_quad, prev % n_quad
        ppar = (pphase + 1) % 2
        go_prev = jnp.logical_and(step > 0, pphase < n_conv - 1)
        cur, nxt = xbs[side], xbs[1 - side]
        gcol = nlayer + (COL_G2 - COL_G1) * nconv + COL_G1
        scol = nlayer + (COL_S2 - COL_S1) * nconv + COL_S1

        if side == 0:
            @pl.when(q == 0)
            def _():
                for idx in range(n_conv):
                    pl.when(phase == idx)(lambda: w_load(idx).wait())
                transpose_weight(raw.at[conv], wt)
                for idx in range(n_conv - 1):
                    pl.when(phase == idx)(lambda: w_load(idx + 2).start())

        @pl.when(conv == 1)
        def _():
            for copy in out_copies(h0_hbm, q):
                copy.wait()

        for pos, row in enumerate(order):
            if pos == 1:
                pl.when(step > 0)(lambda: start_outputs(prev))

                @pl.when(nphase < n_conv)
                def _():
                    wait_stats(nphase % 2, nq)

                @pl.when(nphase > 0)
                def _():
                    wait_halo(nconv, nq)

                make_scale(nphase % 2, nq, gcol, scol, nlayer * n_quad + nq, nconv == 1)
                pack_stats(stats[1 - side], ppar, pq)
            if pos == 2:
                @pl.when(go_prev)
                def _():
                    pair_copy(ppar, pq).start()
            if pos == 3:
                send_halo(1 - conv, q)

                @pl.when(go_prev)
                def _():
                    pair_copy(ppar, pq).wait_recv()
                    add_pair(ppar, pq)
                    send_stats(ppar, pq)
            if pos >= 2:
                half = (rows + 2) // 2
                for nrow in range(half * (pos - 2), half * (pos - 1)):
                    norm_row(nconv, nq, nrow, nxt)
            if pos == 0:
                finish(prev, rows - 1, stats[1 - side])
            else:
                finish(step, pos - 1, stats[side])
            accs[pos % 2][...] = jnp.dot(wt[:, : 3 * kk], cur[row * kk : (row + 3) * kk, :], preferred_element_type=F32)

    @pl.loop(0, n_step // 2)
    def _(pair):
        slot(2 * pair, 0)
        slot(2 * pair + 1, 1)

    finish(n_step - 1, rows - 1, stats[1])
    start_outputs(n_step - 1)

    w_load(n_conv).wait()
    transpose_weight(raw.at[n_conv % 2], wt)
    wt_out = pltpu.make_async_copy(wt, wt_hbm, wt_sem)
    wt_out.start()

    def halo_out(q):
        return pltpu.make_async_copy(act.at[0, q, 0], halo_hbm.at[q], d_sem.at[q])

    for q in range(n_quad):
        if q > 0:
            wait_halo(0, q)
        halo_out(q).start()
    for q in range(n_quad):
        halo_out(q).wait()
        for copy in out_copies(h2_hbm, q):
            copy.wait()
    wt_out.wait()


def down_kernel(
    axis, h0_hbm, h1_hbm, h2_hbm, halo_hbm, w_hbm, par_ref,
    o0_hbm, o1_hbm, o2_hbm, d_hbm,
    b0, b1, b2, halo, w, xb0, xb1, acc_a, acc_b, dbuf, bc, in_sem, halo_sem, w_sem, out_sem, d_sem,
):
    batch, rows, chan, cols = b2.shape
    n_quad = batch // QUAD
    kk = 3 * chan
    chunk = 80
    has_above = lax.axis_index(axis) > 0
    srcs, bufs, outs = (h2_hbm, h0_hbm, h1_hbm), (b2, b0, b1), (o2_hbm, o0_hbm, o1_hbm)
    xbs = (xb0, xb1)
    accs = (acc_a, acc_b)

    def load(which, q):
        part = pl.ds(q * QUAD, QUAD)
        return pltpu.make_async_copy(srcs[which].at[part], bufs[which].at[part], in_sem.at[which, q])

    def save(which, q):
        part = pl.ds(q * QUAD, QUAD)
        return pltpu.make_async_copy(bufs[which].at[part], outs[which].at[part], out_sem.at[which, q])

    def d_copy(q):
        part = pl.ds(q * QUAD, QUAD)
        return pltpu.make_async_copy(dbuf.at[part], d_hbm.at[part], d_sem.at[q])

    halo_load = pltpu.make_async_copy(halo_hbm, halo, halo_sem)
    w_load = pltpu.make_async_copy(w_hbm, w, w_sem)
    halo_load.start()
    load(0, 0).start()
    w_load.start()
    for q in range(1, n_quad):
        load(0, q).start()
    for q in range(n_quad):
        load(1, q).start()
        load(2, q).start()
    bc[...] = jnp.broadcast_to(par_ref[:, COL_BDOWN : COL_BDOWN + 1], (chan, cols))
    pick = lax.broadcasted_iota(jnp.int32, (cols // 2, cols), 1) == 2 * lax.broadcasted_iota(jnp.int32, (cols // 2, cols), 0)
    pick = pick.astype(F32).astype(BF16)

    def build(q, dst, first, last):
        for row in range(first, last):
            for k in range(QUAD):
                for c0 in range(0, chan, chunk):
                    if row == 0:
                        val = halo[q, c0 : c0 + chunk, k * cols : (k + 1) * cols]
                        val = jnp.where(has_above, val.astype(F32), 0.0).astype(BF16)
                    else:
                        val = b2[q * QUAD + k, row - 1, c0 : c0 + chunk, :]
                    store_shifts(dst, row * kk + c0, chan, k, val)

    def finish(q, row, acc):
        for k in range(QUAD):
            full = (acc[:, k * cols : (k + 1) * cols] + bc[...]).astype(BF16)
            picked = lax.dot_general(pick, full, (((1,), (1,)), ((), ())), preferred_element_type=F32)
            dbuf[q * QUAD + k, row] = picked.astype(BF16)

    def product(src, row, acc):
        acc[...] = jnp.dot(w[:, : 3 * kk], src[2 * row * kk : (2 * row + 3) * kk, :], preferred_element_type=F32)

    halo_load.wait()
    load(0, 0).wait()
    save(0, 0).start()
    build(0, xb0, 0, rows + 1)
    w_load.wait()
    half = (rows + 1) // 2

    @pl.loop(0, n_quad // 2)
    def _(pair):
        for side in range(2):
            q = 2 * pair + side
            nq = jnp.minimum(q + 1, n_quad - 1)
            pq = jnp.maximum(q - 1, 0)

            @pl.when(q + 1 < n_quad)
            def _():
                load(0, q + 1).wait()
                save(0, q + 1).start()

            for row in range(rows // 2):
                build(nq, xbs[1 - side], row * half, (row + 1) * half if row == 0 else rows + 1)
                if row == 0:
                    finish(pq, rows // 2 - 1, accs[(rows // 2 - 1) % 2])
                else:
                    finish(q, row - 1, accs[(row - 1) % 2])
                product(xbs[side], row, accs[row % 2])
                load(row + 1, q).wait()
                save(row + 1, q).start()
                if row == 0:
                    pl.when(q > 0)(lambda: d_copy(pq).start())

    finish(n_quad - 1, rows // 2 - 1, accs[(rows // 2 - 1) % 2])
    d_copy(n_quad - 1).start()

    @pl.loop(0, n_quad)
    def _(q):
        for which in range(3):
            save(which, q).wait()
        d_copy(q).wait()


def solution(mesh):
    n_sp = mesh.shape["sp"]

    def band_program(latent, time_emb, w_in, b_in, gn1_scale, gn1_shift, conv1_w, conv1_b, temb_w, temb_b, gn2_scale, gn2_shift, conv2_w, conv2_b, down_w, down_b):
        batch, rows, cols, lat_ch = latent.shape
        chan = w_in.shape[-1]
        layers = conv1_w.shape[0]
        n_quad = batch // QUAD
        lanes = QUAD * cols
        kk = 3 * chan

        lat = latent.reshape(n_quad, QUAD, rows, cols, lat_ch).transpose(0, 2, 4, 1, 3).reshape(n_quad, rows, lat_ch, lanes)
        lat = jnp.pad(lat, ((0, 0), (0, 0), (0, LATENT_PAD - lat_ch), (0, 0)))
        win = jnp.pad(w_in, ((0, 0), (0, 0), (0, LATENT_PAD - lat_ch), (0, 0))).reshape(9 * LATENT_PAD, chan).T
        w1, w2, wd = conv1_w.reshape(layers, 9 * chan, chan), conv2_w.reshape(layers, 9 * chan, chan), down_w.reshape(9 * chan, chan)
        padded = 128 * pl.cdiv(9 * chan, 128)
        par = jnp.concatenate([b_in[None], gn1_scale, gn1_shift, conv1_b, gn2_scale, gn2_shift, conv2_b, down_b[None]], axis=0).astype(F32).T
        emb_act = jax.nn.silu(time_emb.astype(F32)).astype(BF16)
        emb = jnp.einsum("bt,ltc->lbc", emb_act, temb_w, preferred_element_type=F32) + temb_b.astype(F32)[:, None, :]
        emb = emb.reshape(layers * n_quad, QUAD, chan).transpose(0, 2, 1)
        band = jax.ShapeDtypeStruct((batch, rows, chan, cols), BF16)
        hbm = pl.BlockSpec(memory_space=pl.ANY)
        vmem = pl.BlockSpec(memory_space=pltpu.VMEM)
        dma = pltpu.SemaphoreType.DMA
        h0, h1, h2, halo, wt = pl.pallas_call(
            functools.partial(band_kernel, n_sp, "sp"),
            out_shape=(band, band, band, jax.ShapeDtypeStruct((n_quad, chan, lanes), BF16), jax.ShapeDtypeStruct((chan, padded), BF16)),
            in_specs=[hbm, vmem, hbm, hbm, hbm, vmem, vmem],
            out_specs=(hbm,) * 5,
            scratch_shapes=[
                pltpu.VMEM((n_quad, rows + 4, LATENT_PAD, lanes), BF16),
                pltpu.VMEM(((rows + 4) * 3 * LATENT_PAD, lanes), BF16),
                pltpu.VMEM((2, n_quad, rows + 2, chan, lanes), BF16),
                pltpu.VMEM(((rows + 2) * kk, lanes), BF16),
                pltpu.VMEM(((rows + 2) * kk, lanes), BF16),
                pltpu.VMEM((2, padded, chan), BF16),
                pltpu.VMEM((chan, padded), BF16),
                pltpu.VMEM((chan, lanes), F32),
                pltpu.VMEM((chan, lanes), F32),
                pltpu.VMEM((N_COLS, chan, cols), F32),
                pltpu.VMEM((2 * QUAD, chan, cols), F32),
                pltpu.VMEM((2 * QUAD, chan, cols), F32),
                pltpu.VMEM((QUAD, chan, cols), F32),
                pltpu.VMEM((QUAD, chan, cols), F32),
                pltpu.VMEM((QUAD, chan, cols), F32),
                pltpu.VMEM((QUAD, chan, cols), F32),
                pltpu.VMEM((2, n_quad, 2 * QUAD, cols), F32),
                pltpu.VMEM((2, n_quad, 2 * QUAD, cols), F32),
                pltpu.VMEM((2, n_quad, 2 * QUAD, cols), F32),
                pltpu.VMEM((2, n_quad, n_sp // CORES - 1, 2 * QUAD, cols), F32),
                dma, dma((2,)), dma, dma((n_quad, QUAD)), dma((n_quad,)),
                dma((2,)), dma((2,)), dma((2, n_quad)), dma((2, n_quad)), dma((2, n_quad)), dma((2, n_quad)),
                dma((2, n_quad, 2)), dma((2, n_quad, 2)),
            ],
            compiler_params=pltpu.CompilerParams(collective_id=0, has_side_effects=True, vmem_limit_bytes=60 * 1024 * 1024),
            name="band",
        )(lat, win, w1, w2, wd, par, emb)
        h0, h1, h2, d = pl.pallas_call(
            functools.partial(down_kernel, "sp"),
            out_shape=(band, band, band, jax.ShapeDtypeStruct((batch, rows // 2, cols // 2, chan), BF16)),
            in_specs=[hbm] * 5 + [vmem],
            out_specs=(hbm,) * 4,
            scratch_shapes=[
                pltpu.VMEM(band.shape, BF16), pltpu.VMEM(band.shape, BF16), pltpu.VMEM(band.shape, BF16),
                pltpu.VMEM((n_quad, chan, lanes), BF16),
                pltpu.VMEM((chan, padded), BF16),
                pltpu.VMEM(((rows + 1) * kk, lanes), BF16),
                pltpu.VMEM(((rows + 1) * kk, lanes), BF16),
                pltpu.VMEM((chan, lanes), F32),
                pltpu.VMEM((chan, lanes), F32),
                pltpu.VMEM((batch, rows // 2, cols // 2, chan), BF16),
                pltpu.VMEM((chan, cols), F32),
                dma((3, n_quad)), dma, dma, dma((3, n_quad)), dma((n_quad,)),
            ],
            compiler_params=pltpu.CompilerParams(vmem_limit_bytes=60 * 1024 * 1024),
            name="down",
        )(h0, h1, h2, halo, wt, par)
        return tuple(h.transpose(0, 1, 3, 2) for h in (h0, h1, h2)) + (d,)

    band_spec = P("dp", "sp", None, None)
    return jax.shard_map(band_program, mesh=mesh, in_specs=(band_spec, P("dp", None)) + (P(),) * 14, out_specs=(band_spec,) * 4, check_vma=False)
```

time: 220 us -> 151 us (0.69)
  Pallas kernels: 178 us -> 138 us
  local copies, waits for them, and re-layouts: 38 us -> 9.28 us
    pallas_call x1, Pallas kernels: 178 us -> 119 us  [band_program(): pl.pallas_call(functools.partial(band_kernel, n_sp, 'sp'), out_shape=(ban...]
    pallas_call x0 -> x1, Pallas kernels: none -> 19.7 us  [band_program(): pl.pallas_call(functools.partial(down_kernel, 'sp'), out_shape=(band, ban...]
    reshape x3 -> x0, local copies, waits for them, and re-layouts: 16.5 us -> none  [the longest x1 6.23 us: band_program(): w1 = conv1_w.reshape(layers, 9 * chan, chan).transpose(0, 2, 1)]
    unnamed x14 -> x2, local copies, waits for them, and re-layouts: 13 us -> 0.01 us
where the time goes in v2:
time: 151 us
  Pallas kernels  138 us (91%)
  local copies, waits for them, and re-layouts  9.28 us (6%)
    pallas_call x1, Pallas kernels, band_program(): pl.pallas_call(functools.partial(band_kernel, n_sp, 'sp'), out_shape=(ban...  119 us
    pallas_call x1, Pallas kernels, band_program(): pl.pallas_call(functools.partial(down_kernel, 'sp'), out_shape=(band, ban...  19.7 us

profile of v2, /device:TPU:97, one launch (start us, length us, event | category | flops | bytes accessed | tf_op | source)
XLA Modules:
  0.0 150.5 jit_solution(13948774236171376043)
XLA Ops:
  0.6 0.0 copy-start
  0.6 0.8 broadcast_in_dim.7
  1.5 0.7 broadcast_in_dim.8
  2.1 0.7 convert_element_type.16
  2.8 2.2 %concatenate.3 = bf16[14,320]{1,0:T(8,128)(2,1)S(1)} concatenate(bf16[1,320]{1,0:T(2,128)(2,1)S(1)} %broadcast_in_dim.7, bf16[2,320]{1,0:T(2,128)(2,1)} %param.20, bf16[2,320]{1,0:T(2,128)(2,1)} %param.21, bf16[2,320]{1,0:T(2,128)(2,1)} %param.23, bf16[2,320]{1,0:T(2,128)(2,1)} %param.26, bf16[2,320]{1,0:T(2,128)(2,1)} %param.27, bf16[2,320]{1,0:T(2,128)(2,1)} %param.29, ...), dimensions={0} | concatenate | bytes 17920 | tf_op jit(solution)/shard_map/concatenate | solution.py:484
  5.1 0.0 copy-done
  5.1 1.3 fusion
  6.5 0.9 copy.44
  7.4 0.8 pad.9
  8.1 0.8 copy.40
  8.9 0.8 copy.41
  9.7 0.7 pad.8.lat_hbm
  10.5 1.5 %copy.42 = f32[8,4,320]{1,2,0:T(8,128)} copy(f32[8,4,320]{2,1,0:T(4,128)S(1)} %reshape.36) | data formatting | bytes 81920 | tf_op jit(solution)/shard_map/reshape | solution.py:487
  12.0 118.7 %band.1 = (bf16[16,4,320,128]{3,2,1,0:T(8,128)(2,1)}, bf16[16,4,320,128]{3,2,1,0:T(8,128)(2,1)}, bf16[16,4,320,128]{3,2,1,0:T(8,128)(2,1)}, bf16[4,320,512]{2,1,0:T(8,128)(2,1)}, bf16[320,2944]{1,0:T(8,128)(2,1)}) custom-call(bf16[4,4,16,512]{3,2,1,0:T(8,128)(2,1)} %pad.8.lat_hbm, bf16[320,144]{1,0:T(8,128)(2,1)} %bitcast.26, ...), custom_call_target="tpu_custom_call" | custom-call | tf_op jit(solution)/shard_map/band/pallas_call | solution.py:492
  130.7 19.7 %down.1 = (bf16[16,4,320,128]{3,2,1,0:T(8,128)(2,1)}, bf16[16,4,320,128]{3,2,1,0:T(8,128)(2,1)}, bf16[16,4,320,128]{3,2,1,0:T(8,128)(2,1)}, bf16[16,2,64,320]{3,2,1,0:T(8,128)(2,1)}) custom-call(bf16[16,4,320,128]{3,2,1,0:T(8,128)(2,1)} %get-tuple-element.13.h0_hbm, bf16[16,4,320,128]{3,2,1,0:T(8,128)(2,1)} %get-tuple-element.14.h1_hbm, ...), custom_call_target="tpu_custom_call" | custom-call | tf_op jit(solution)/shard_map/down/pallas_call | solution.py:525
  (2 shorter events, 0.1 us)
Async XLA Ops:
  0.6 4.4 %copy-start = (bf16[2,1280,320]{1,2,0:T(8,128)(2,1)S(1)}, bf16[2,1280,320]{1,2,0:T(8,128)(2,1)}, u32[]{:S(2)}) copy-start(bf16[2,1280,320]{1,2,0:T(8,128)(2,1)} %param.24) | copy-start | bytes 4915204
